TPU v7x, 256 devices: a whole 4x4x8 slice. The times are simulated.
256 devices in a mesh: parts: 256 (over y, x, z, core).
Axes of the slice: x: 4, y: 4, z: 8, core: 2. Of those that a mesh axis runs over, the one named last changes fastest.
Arguments:
- basis: float32 [16, 262144], P(None, 'parts'), may hold values from -8000 to 8000, as said below
- k_tiles: float32 [2048, 5, 128, 128], P('parts'), may hold values from -3 to 11, as said below
- m_tiles: float32 [2048, 5, 128, 128], P('parts'), may hold values from -2 to 4, as said below
- tile_part: int32 [2048, 5], P('parts'), may hold values from 0 to 255, as said below
- tile_slot: int32 [2048, 5], P('parts'), may hold values from 0 to 7, as said below
- iface_rows: int32 [512], P('parts'), may hold values from 0 to 7
Outputs:
- corrections: float32 [16, 262144], P(None, 'parts')
- theta: float32 [16], replicated
Inputs may be any that keep to these rules, and one draw needn't show every extreme that they name: `basis`: the rows form a full-rank set. `k_tiles`: block 0 of every row tile has a positive diagonal well above its other entries. `m_tiles`: block 0 of every row tile has a positive diagonal. `tile_part`: block 0 of a row tile lies in its own partition; every other block lies in its own partition, in the partition 1 away on either side, or in the partition 128 away, counted modulo the number of partitions. `tile_slot`: where the block lies in the own partition this is a row tile of it (for block 0 the row tile itself); elsewhere an interface slot below 2.
All inputs are finite; a program needn't handle non-finite values.
Results may differ from a plain program's by a relative error of at most 0.0003.
Values sent between devices are 32-bit elements; how exact they have to be, the bound alone decides.
A program may use at most 64 MiB of HBM per device.

v0:
```python
import functools

import jax
import jax.numpy as jnp
from jax import lax
from jax.experimental import pallas as pl
from jax.experimental.pallas import tpu as pltpu
from jax.sharding import PartitionSpec as P

AXIS = "parts"
PARTS = 256
GROUP = 16
FAR = 128
PAIRS = 16
TILES = 8
BLOCKS = 5
WIDTH = 128
LOCAL = TILES * WIDTH
EXT = TILES + 6
RELAX = 0.4
MESH = pl.DeviceIdType.MESH
F32 = jnp.float32
BF16 = jnp.bfloat16
NT = (((1,), (1,)), ((), ()))
TN = (((0,), (0,)), ((), ()))


def split(x):
    hi = x.astype(BF16)
    return hi, (x - hi.astype(F32)).astype(BF16)


def mm(a, b):
    return jnp.dot(a, b, preferred_element_type=F32)


def mm_nt(a, b):
    return lax.dot_general(a, b, NT, preferred_element_type=F32)


def small(a, b, dims=(((1,), (0,)), ((), ()))):
    return lax.dot_general(
        a, b, dims, precision=lax.Precision.HIGHEST, preferred_element_type=F32
    )


def pack4(v):
    return jnp.concatenate([v[4 * i : 4 * i + 4] for i in range(4)], axis=1)


def unpack4(v):
    return jnp.concatenate([v[:, 32 * i : 32 * i + 32] for i in range(4)], axis=0)


def eliminate(gram, rows, eye):
    aug = jnp.concatenate([gram, eye], axis=1)
    for j in range(PAIRS):
        pivot = aug[j : j + 1, j : j + 1]
        d = lax.rsqrt(pivot)
        d = d * (1.5 - 0.5 * pivot * d * d)
        line = aug[j : j + 1, :] * d
        col = aug[:, j : j + 1] * d
        aug = jnp.where(rows == j, line, jnp.where(rows > j, aug - col * line, aug))
    return aug[:, PAIRS:]


def kernel(
    scale,
    basis_ref,
    k_ref,
    m_ref,
    part_ref,
    slot_ref,
    iface_ref,
    out_ref,
    theta_ref,
    kbuf,
    mbuf,
    w_hi,
    w_lo,
    xt,
    dinv,
    ext16,
    ext32,
    words,
    words_r,
    s_hi,
    s_lo,
    pt,
    ad,
    right,
    left,
    h0out,
    h1out,
    h2out,
    h3out,
    h0in,
    h1in,
    h2in,
    h3in,
    ar_big,
    ar_small,
    load_sem,
    x_sem,
    hs_sem,
    hr_sem,
    as_sem,
    ar_sem,
):
    me = lax.axis_index(AXIS)
    rank_a = lax.rem(me, GROUP)
    base_a = me - rank_a
    rank_b = me // GROUP
    halo_to = (
        lax.rem(me + PARTS - 1, PARTS),
        lax.rem(me + 1, PARTS),
        lax.rem(me + FAR, PARTS),
    )

    def peer_a(k):
        return base_a + lax.rem(rank_a + k, GROUP)

    def peer_b(k):
        return rank_a + GROUP * lax.rem(rank_b + k, GROUP)

    loads = []
    for i in range(TILES):
        loads.append(
            pltpu.make_async_copy(
                basis_ref.at[:, pl.ds(i * WIDTH, WIDTH)], xt.at[i], x_sem.at[i]
            )
        )
        loads[-1].start()
    for i in range(TILES):
        for n, (src, dst) in enumerate(((k_ref, kbuf), (m_ref, mbuf))):
            pltpu.make_async_copy(src.at[i], dst.at[i], load_sem.at[n, i]).start()

    barrier = pltpu.get_barrier_semaphore()

    def greet(k, carry):
        pl.semaphore_signal(barrier, inc=1, device_id=(peer_a(k),), device_id_type=MESH)
        pl.semaphore_signal(barrier, inc=1, device_id=(peer_b(k),), device_id_type=MESH)
        return carry

    lax.fori_loop(1, GROUP, greet, 0)
    for device in halo_to:
        pl.semaphore_signal(barrier, inc=1, device_id=(device,), device_id_type=MESH)

    def halo(step, out, into):
        for g, device in enumerate(halo_to):
            pltpu.make_async_remote_copy(
                src_ref=out,
                dst_ref=into.at[g],
                send_sem=hs_sem.at[step],
                recv_sem=hr_sem.at[step],
                device_id=(device,),
                device_id_type=MESH,
            ).start()

    def halo_wait(step, into):
        pltpu.make_async_copy(into, into, hr_sem.at[step]).wait()

    def spread(buf, stage, step, value):
        rank = rank_a if stage == 0 else rank_b
        peer = peer_a if stage == 0 else peer_b
        buf[rank] = value

        def send(k, carry):
            pltpu.make_async_remote_copy(
                src_ref=buf.at[rank],
                dst_ref=buf.at[rank],
                send_sem=as_sem.at[2 * step + stage],
                recv_sem=ar_sem.at[2 * step + stage],
                device_id=(peer(k),),
                device_id_type=MESH,
            ).start()
            return carry

        lax.fori_loop(1, GROUP, send, 0)

    def gathered(buf, stage, step):
        most = buf.at[pl.ds(0, GROUP - 1)]
        pltpu.make_async_copy(most, most, ar_sem.at[2 * step + stage]).wait()
        total = buf[0]
        for j in range(1, GROUP):
            total = total + buf[j]
        return total

    columns = []
    for i in range(TILES):
        line = []
        for b in range(BLOCKS):
            part = part_ref[i, b]
            slot = slot_ref[i, b]
            where = jnp.where(
                part == halo_to[1],
                TILES,
                jnp.where(part == halo_to[0], TILES + 2, TILES + 4),
            )
            line.append(jnp.where(part == me, slot, where + slot))
        columns.append(line)
    iface = [iface_ref[0], iface_ref[1]]

    def span(i):
        return pl.ds(i * WIDTH, WIDTH)

    for copy in loads:
        copy.wait()
    for s in range(2):
        h0out[s] = xt[iface[s]]
    pl.semaphore_wait(barrier, 33)
    halo(0, h0out, h0in)

    eye_w = lax.broadcasted_iota(jnp.int32, (WIDTH, WIDTH), 0) == lax.broadcasted_iota(
        jnp.int32, (WIDTH, WIDTH), 1
    )
    for i in range(TILES):
        hi, lo = split(xt[i])
        ext16[i, 0:16] = hi
        ext16[i, 16:32] = lo
        right[64:80, span(i)] = hi
        right[80:96, span(i)] = lo
        left[0:16, span(i)] = hi
        left[48:64, span(i)] = lo

    def prepare(i, carry):
        for n, (src, dst) in enumerate(((k_ref, kbuf), (m_ref, mbuf))):
            pltpu.make_async_copy(src.at[i], dst.at[i], load_sem.at[n, i]).wait()
            for b in range(BLOCKS):
                hi, lo = split(dst[i, b].T)
                w_hi[i, b * WIDTH : (b + 1) * WIDTH, n * WIDTH : (n + 1) * WIDTH] = hi
                w_lo[i, b * WIDTH : (b + 1) * WIDTH, n * WIDTH : (n + 1) * WIDTH] = lo
        diagonal = jnp.sum(jnp.where(eye_w, kbuf[i, 0], 0.0), axis=0, keepdims=True)
        dinv[i] = jnp.broadcast_to(1.0 / diagonal, (8, WIDTH))
        return carry

    lax.fori_loop(0, TILES, prepare, 0)
    d = [dinv[i, 0:1] for i in range(TILES)]
    for i in range(TILES):
        hi, lo = split(xt[i] * d[i])
        right[16:32, span(i)] = hi
        right[48:64, span(i)] = lo

    def apply(ext, rows, i):
        picked = jnp.concatenate([ext[columns[i][b]] for b in range(BLOCKS)], axis=1)
        high = mm(picked, w_hi[i])
        low = mm(picked[:rows], w_lo[i])
        return high[:rows] + high[rows:] + low

    halo_wait(0, h0in)
    for g in range(3):
        for s in range(2):
            hi, lo = split(h0in[g, s])
            ext16[TILES + 2 * g + s, 0:16] = hi
            ext16[TILES + 2 * g + s, 16:32] = lo
    for i in range(TILES):
        y = apply(ext16, 16, i)
        p, q = y[:, :WIDTH], y[:, WIDTH:]
        words[i, 0:16] = p * d[i]
        words[i, 16:32] = q * d[i]
        hi, lo = split(p)
        left[16:32, span(i)] = hi
        left[64:80, span(i)] = lo
        hi, lo = split(q)
        left[32:48, span(i)] = hi
        left[80:96, span(i)] = lo
        right[0:16, span(i)] = hi
        right[32:48, span(i)] = lo
    for s in range(2):
        h1out[s] = words[iface[s], 0:32]
    halo(1, h1out, h1in)

    gram = mm_nt(left[0:96], right[...])
    gram = gram[0:48] + gram[48:96]
    with_qx = gram[:, 0:32] + gram[:, 32:64]
    with_x = gram[:, 64:80] + gram[:, 80:96]
    payload = jnp.concatenate(
        [with_qx[16:32], with_qx[32:48], with_x[0:16], jnp.zeros((16, 48), F32)], axis=1
    )
    spread(ar_big.at[0], 0, 0, payload)

    for i in range(TILES):
        hi, lo = split(words[i, 0:32])
        ext32[i, 0:32] = hi
        ext32[i, 32:64] = lo
        s_hi[i, 0:32] = hi
        s_lo[i, 0:32] = lo
    spread(ar_big.at[1], 1, 0, gathered(ar_big.at[0], 0, 0))
    halo_wait(1, h1in)
    for g in range(3):
        for s in range(2):
            hi, lo = split(h1in[g, s])
            t = TILES + 2 * g + s
            ext32[t, 0:32] = hi
            ext32[t, 32:64] = lo
            s_hi[t, 0:32] = hi
            s_lo[t, 0:32] = lo

    for i in range(TILES):
        y = apply(ext32, 32, i)
        stiff, mass = y[:, :WIDTH], y[:, WIDTH:]
        hi, lo = split(stiff)
        left[0:32, span(i)] = hi
        left[64:96, span(i)] = lo
        hi, lo = split(mass)
        left[32:64, span(i)] = hi
        left[96:128, span(i)] = lo
        stiff, mass = stiff * d[i], mass * d[i]
        words[i, 32:48] = stiff[16:32]
        words[i, 48:64] = mass[16:32]
        words[i, 64:80] = stiff[0:16]
        words[i, 80:96] = mass[0:16]
    for s in range(2):
        h2out[s] = words[iface[s], 32:96]
    halo(2, h2out, h2in)
    gram = mm_nt(left[...], right[0:64])
    gram = gram[0:64] + gram[64:128]
    gram = gram[:, 0:32] + gram[:, 32:64]
    payload = jnp.concatenate([gram[16 * r : 16 * r + 16] for r in range(4)], axis=1)
    spread(ar_big.at[2], 0, 1, payload)
    for i in range(TILES):
        hi, lo = split(words[i, 32:96])
        s_hi[i, 32:96] = hi
        s_lo[i, 32:96] = lo

    total = gathered(ar_big.at[1], 1, 0) * scale
    g_p, g_q, g_xx = total[:, 0:32], total[:, 32:64], total[:, 64:80]
    g_pq, g_px = g_p[:, 0:16], g_p[:, 16:32]
    g_qq, g_qx = g_q[:, 0:16], g_q[:, 16:32]
    row_no = lax.broadcasted_iota(jnp.int32, (PAIRS, 2 * PAIRS), 0)
    eye_b = lax.broadcasted_iota(jnp.int32, (PAIRS, PAIRS), 0) == lax.broadcasted_iota(
        jnp.int32, (PAIRS, PAIRS), 1
    )
    eye = jnp.where(eye_b, 1.0, 0.0).astype(F32)
    inv_v = eliminate(g_xx, row_no, eye)
    inv_m = eliminate(g_qq, row_no, eye)
    projected = small(inv_m, g_pq, NT)
    diag_v = jnp.sum(jnp.where(eye_b, inv_v, 0.0), axis=1, keepdims=True)
    diag_m = jnp.sum(jnp.where(eye_b, inv_m, 0.0), axis=1, keepdims=True)
    theta = jnp.sum(projected * inv_v, axis=1, keepdims=True) * diag_m / diag_v
    theta_ref[...] = jnp.sum(jnp.where(eye_b, theta, 0.0), axis=0, keepdims=True)
    wide = jnp.broadcast_to(theta, (PAIRS, WIDTH))
    gram_v = small(inv_v, inv_v, TN)
    gram_m = small(inv_m, inv_m, TN)
    start_p = -RELAX * inv_v
    start_q = RELAX * theta * inv_v
    start_x = small(start_p, g_px) + small(start_q, g_qx)
    r = small(start_x, gram_v)
    r_pq = small(r, g_pq)
    coef = jnp.concatenate(
        [
            2.0 * start_p + RELAX * r,
            2.0 * start_q,
            -RELAX * start_q,
            RELAX * theta * start_q,
            -RELAX * start_p,
            RELAX * theta * start_p,
        ],
        axis=1,
    )
    spread(ar_big.at[3], 1, 1, gathered(ar_big.at[2], 0, 1))
    halo_wait(2, h2in)
    for g in range(3):
        for s in range(2):
            hi, lo = split(h2in[g, s])
            t = TILES + 2 * g + s
            s_hi[t, 32:96] = hi
            s_lo[t, 32:96] = lo

    def combine(coef, rows, t):
        hi, lo = split(coef)
        both = jnp.concatenate([hi, lo], axis=0)
        first = mm(both, s_hi[t, 0:rows])
        second = mm(hi, s_lo[t, 0:rows])
        return first[0:16] + first[16:32] + second

    for t in range(EXT):
        p = combine(coef, 96, t)
        pt[t] = p
        hi, lo = split(p)
        ext16[t, 0:16] = hi
        ext16[t, 16:32] = lo

    def residual(step, last):
        for i in range(TILES):
            y = apply(ext16, 16, i)
            image = y[:, :WIDTH] - wide * y[:, WIDTH:]
            hi, lo = split(image)
            left[0:16, span(i)] = hi
            left[16:32, span(i)] = lo
            ad[i] = image * d[i]
        if not last:
            out = h3out.at[step - 1]
            for s in range(2):
                out[s] = ad[iface[s]]
            halo(step + 2, out, h3in.at[step - 1])
        gram = mm_nt(left[0:32], right[0:64])
        gram = gram[0:16] + gram[16:32]
        gram = gram[:, 0:32] + gram[:, 32:64]
        spread(ar_small.at[2 * step - 2], 0, step + 1, pack4(gram))

    residual(1, False)

    total = gathered(ar_big.at[3], 1, 1) * scale
    kq, mq = total[:, 32:64], total[:, 96:128]
    kp, mp = total[:, 0:32], total[:, 64:96]
    image = (small(start_p, kp) + small(start_q, kq)) - theta * (
        small(start_p, mp) + small(start_q, mq)
    )
    p_x = 2.0 * start_x - RELAX * image[:, 16:32] + RELAX * small(r, g_px)

    for step in (1, 2, 3):
        m = small(image[:, 0:16] - r_pq, gram_m)
        c_x = p_x + RELAX * small(m, g_qx)
        r = small(c_x, gram_v)
        m_image = RELAX * (small(m, kq) - theta * small(m, mq))
        coef = jnp.concatenate(
            [
                start_p + RELAX * r,
                start_q + RELAX * m,
                -RELAX * RELAX * m,
                RELAX * RELAX * theta * m,
            ],
            axis=1,
        )
        if step < 3:
            for t in range(TILES):
                p = pt[t] - RELAX * ad[t] + combine(coef, 64, t)
                pt[t] = p
                hi, lo = split(p)
                ext16[t, 0:16] = hi
                ext16[t, 16:32] = lo
            for t in range(TILES, EXT):
                pt[t] = pt[t] + combine(coef, 64, t)
            got = gathered(ar_small.at[2 * step - 2], 0, step + 1)
            spread(ar_small.at[2 * step - 1], 1, step + 1, got)
            halo_wait(step + 2, h3in.at[step - 1])
            for g in range(3):
                for s in range(2):
                    t = TILES + 2 * g + s
                    p = pt[t] - RELAX * h3in[step - 1, g, s]
                    pt[t] = p
                    hi, lo = split(p)
                    ext16[t, 0:16] = hi
                    ext16[t, 16:32] = lo
            residual(step + 1, step == 2)
        else:
            got = gathered(ar_small.at[2 * step - 2], 0, step + 1)
            spread(ar_small.at[2 * step - 1], 1, step + 1, got)
            for t in range(TILES):
                pt[t] = pt[t] - RELAX * ad[t] + combine(coef, 64, t)
        r_px = small(r, g_px)
        r_pq = small(r, g_pq)
        total = unpack4(gathered(ar_small.at[2 * step - 1], 1, step + 1)) * scale
        image = total + m_image
        p_x = c_x + start_x - RELAX * image[:, 16:32] + RELAX * r_px

    m = small(image[:, 0:16] - r_pq, gram_m)
    c_x = p_x + RELAX * small(m, g_qx)
    r = small(c_x, gram_v)
    q_hi, q_lo = split(RELAX * m)
    x_hi, x_lo = split(-r)
    lead = jnp.concatenate([q_hi, x_hi], axis=1)
    rest = jnp.concatenate([q_lo, x_lo], axis=1)
    for t in range(TILES):
        hi = jnp.concatenate([s_hi[t, 16:32], right[64:80, span(t)]], axis=0)
        lo = jnp.concatenate([s_lo[t, 16:32], right[80:96, span(t)]], axis=0)
        out_ref[:, span(t)] = pt[t] + (mm(lead, hi) + mm(rest, hi) + mm(lead, lo))

    for step, out in enumerate((h0out, h1out, h2out, h3out.at[0], h3out.at[1])):
        for g in range(3):
            pltpu.make_async_copy(out, out, hs_sem.at[step]).wait()
    for step in range(5):
        for stage in range(2):
            buf = ar_big.at[2 * step + stage] if step < 2 else ar_small.at[2 * step - 4 + stage]
            most = buf.at[pl.ds(0, GROUP - 1)]
            pltpu.make_async_copy(most, most, as_sem.at[2 * step + stage]).wait()


def shards(basis, k_tiles, m_tiles, tile_part, tile_slot, iface_rows):
    rows = basis.shape[1] * lax.axis_size(AXIS)
    vmem = pltpu.VMEM
    corrections, theta = pl.pallas_call(
        functools.partial(kernel, 1.0 / rows),
        out_shape=(
            jax.ShapeDtypeStruct((PAIRS, LOCAL), F32),
            jax.ShapeDtypeStruct((1, PAIRS), F32),
        ),
        in_specs=[pl.BlockSpec(memory_space=pl.ANY)] * 3
        + [pl.BlockSpec(memory_space=pltpu.SMEM)] * 3,
        out_specs=(pl.BlockSpec(memory_space=vmem), pl.BlockSpec(memory_space=vmem)),
        scratch_shapes=[
            vmem((TILES, BLOCKS, WIDTH, WIDTH), F32),
            vmem((TILES, BLOCKS, WIDTH, WIDTH), F32),
            vmem((TILES, BLOCKS * WIDTH, 2 * WIDTH), BF16),
            vmem((TILES, BLOCKS * WIDTH, 2 * WIDTH), BF16),
            vmem((TILES, 16, WIDTH), F32),
            vmem((TILES, 8, WIDTH), F32),
            vmem((EXT, 32, WIDTH), BF16),
            vmem((EXT, 64, WIDTH), BF16),
            vmem((TILES, 96, WIDTH), F32),
            vmem((8, WIDTH), F32),
            vmem((EXT, 96, WIDTH), BF16),
            vmem((EXT, 96, WIDTH), BF16),
            vmem((EXT, 16, WIDTH), F32),
            vmem((TILES, 16, WIDTH), F32),
            vmem((96, LOCAL), BF16),
            vmem((128, LOCAL), BF16),
            vmem((2, 16, WIDTH), F32),
            vmem((2, 32, WIDTH), F32),
            vmem((2, 64, WIDTH), F32),
            vmem((2, 2, 16, WIDTH), F32),
            vmem((3, 2, 16, WIDTH), F32),
            vmem((3, 2, 32, WIDTH), F32),
            vmem((3, 2, 64, WIDTH), F32),
            vmem((2, 3, 2, 16, WIDTH), F32),
            vmem((4, GROUP, 16, WIDTH), F32),
            vmem((6, GROUP, 4, WIDTH), F32),
            pltpu.SemaphoreType.DMA((2, TILES)),
            pltpu.SemaphoreType.DMA((TILES,)),
            pltpu.SemaphoreType.DMA((5,)),
            pltpu.SemaphoreType.DMA((5,)),
            pltpu.SemaphoreType.DMA((10,)),
            pltpu.SemaphoreType.DMA((10,)),
        ],
        compiler_params=pltpu.CompilerParams(
            collective_id=0, has_side_effects=True, vmem_limit_bytes=48 * 1024 * 1024
        ),
    )(basis, k_tiles, m_tiles, tile_part, tile_slot, iface_rows)
    return corrections, theta.reshape(PAIRS)


def solution(mesh):
    in_specs = (
        P(None, AXIS),
        P(AXIS, None, None, None),
        P(AXIS, None, None, None),
        P(AXIS, None),
        P(AXIS, None),
        P(AXIS),
    )
    return jax.shard_map(
        shards, mesh=mesh, in_specs=in_specs, out_specs=(P(None, AXIS), P()), check_vma=False
    )
```

profile of v0, /device:TPU:1, one launch (start us, length us, event | category | flops | bytes accessed | tf_op | source)
XLA Modules:
  0.0 63.9 jit_solution(12845543191790188736)
XLA Ops:
  0.6 0.0 copy-start
  0.6 1.7 %copy-done = f32[8,5,128,128]{3,2,1,0:T(8,128)S(1)} copy-done((f32[8,5,128,128]{3,2,1,0:T(8,128)S(1)}, f32[8,5,128,128]{3,2,1,0:T(8,128)}, u32[]{:S(2)}) %copy-start) | copy-done | bytes 2621464
  2.4 0.0 copy-start.1
  2.4 1.7 %copy-done.1 = f32[8,5,128,128]{3,2,1,0:T(8,128)S(1)} copy-done((f32[8,5,128,128]{3,2,1,0:T(8,128)S(1)}, f32[8,5,128,128]{3,2,1,0:T(8,128)}, u32[]{:S(2)}) %copy-start.1) | copy-done | bytes 2621464
  4.1 0.0 copy-start.2
  4.1 0.8 %copy-done.2 = f32[16,1024]{1,0:T(8,128)S(1)} copy-done((f32[16,1024]{1,0:T(8,128)S(1)}, f32[16,1024]{1,0:T(8,128)}, u32[]{:S(2)}) %copy-start.2) | copy-done | bytes 65560
  5.0 0.0 copy-start.3
  5.0 0.7 %copy-done.3 = s32[8,5]{1,0:T(8,128)S(1)} copy-done((s32[8,5]{1,0:T(8,128)S(1)}, s32[8,5]{1,0:T(8,128)}, u32[]{:S(2)}) %copy-start.3) | copy-done | bytes 184
  5.6 0.0 copy-start.4
  5.6 0.7 %copy-done.4 = s32[8,5]{1,0:T(8,128)S(1)} copy-done((s32[8,5]{1,0:T(8,128)S(1)}, s32[8,5]{1,0:T(8,128)}, u32[]{:S(2)}) %copy-start.4) | copy-done | bytes 184
  6.3 0.0 copy-start.5
  6.3 0.7 %copy-done.5 = s32[2]{0:T(128)S(1)} copy-done((s32[2]{0:T(128)S(1)}, s32[2]{0:T(128)}, u32[]{:S(2)}) %copy-start.5) | copy-done | bytes 32
  7.0 55.8 %shard_map.77 = (f32[16,1024]{1,0:T(8,128)S(1)}, f32[1,16]{1,0:T(1,128)S(1)}) custom-call(f32[16,1024]{1,0:T(8,128)S(1)} %copy-done.2, f32[8,5,128,128]{3,2,1,0:T(8,128)S(1)} %copy-done, f32[8,5,128,128]{3,2,1,0:T(8,128)S(1)} %copy-done.1, s32[8,5]{1,0:T(8,128)S(1)} %copy-done.3, s32[8,5]{1,0:T(8,128)S(1)} %copy-done.4, s32[2]{0:T(128)S(1)} %copy-done.5), custom_call_target="tpu_custom_call" | custom-call | tf_op jit(solution)/shard_map/pallas_call | solution.py:483
  62.8 0.6 copy.10
  63.4 0.5 copy.11
Async XLA Ops:
  0.6 1.7 %copy-start = (f32[8,5,128,128]{3,2,1,0:T(8,128)S(1)}, f32[8,5,128,128]{3,2,1,0:T(8,128)}, u32[]{:S(2)}) copy-start(f32[8,5,128,128]{3,2,1,0:T(8,128)} %k_ref.1) | copy-start | bytes 7864324
  2.4 1.7 %copy-start.1 = (f32[8,5,128,128]{3,2,1,0:T(8,128)S(1)}, f32[8,5,128,128]{3,2,1,0:T(8,128)}, u32[]{:S(2)}) copy-start(f32[8,5,128,128]{3,2,1,0:T(8,128)} %m_ref.1) | copy-start | bytes 7864324
  4.1 0.8 %copy-start.2 = (f32[16,1024]{1,0:T(8,128)S(1)}, f32[16,1024]{1,0:T(8,128)}, u32[]{:S(2)}) copy-start(f32[16,1024]{1,0:T(8,128)} %basis_ref.1) | copy-start | bytes 196612
  5.0 0.7 %copy-start.3 = (s32[8,5]{1,0:T(8,128)S(1)}, s32[8,5]{1,0:T(8,128)}, u32[]{:S(2)}) copy-start(s32[8,5]{1,0:T(8,128)} %part_ref.1) | copy-start | bytes 484
  5.6 0.7 %copy-start.4 = (s32[8,5]{1,0:T(8,128)S(1)}, s32[8,5]{1,0:T(8,128)}, u32[]{:S(2)}) copy-start(s32[8,5]{1,0:T(8,128)} %slot_ref.1) | copy-start | bytes 484
  6.3 0.7 %copy-start.5 = (s32[2]{0:T(128)S(1)}, s32[2]{0:T(128)}, u32[]{:S(2)}) copy-start(s32[2]{0:T(128)} %iface_ref.1) | copy-start | bytes 28
where the time goes:
time: 64.2 us; the launch traced here: 63.9 us
  Pallas kernels  55.8 us (87%)
  local copies, waits for them, and re-layouts  7.48 us (12%)
  between operations  0.65 us (1%)
    pallas_call x1, Pallas kernels, shards(): pl.pallas_call(functools.partial(kernel, 1.0 / rows), out_shape=(jax.Shap...  55.8 us
    unnamed x14, local copies, waits for them, and re-layouts  7.48 us

commit v1 on v0

--- a/solution.py
+++ b/solution.py
@@ -69,9 +69,9 @@
     basis_ref,
     k_ref,
     m_ref,
-    part_ref,
-    slot_ref,
-    iface_ref,
+    part_hbm,
+    slot_hbm,
+    iface_hbm,
     out_ref,
     theta_ref,
     kbuf,
@@ -83,7 +83,6 @@
     ext16,
     ext32,
     words,
-    words_r,
     s_hi,
     s_lo,
     pt,
@@ -98,9 +97,14 @@
     h1in,
     h2in,
     h3in,
+    ar_first,
     ar_big,
     ar_small,
+    part_ref,
+    slot_ref,
+    iface_ref,
     load_sem,
+    index_sem,
     x_sem,
     hs_sem,
     hr_sem,
@@ -123,7 +127,22 @@
     def peer_b(k):
         return rank_a + GROUP * lax.rem(rank_b + k, GROUP)
 
+    barrier = pltpu.get_barrier_semaphore()
+
+    def greet(k, carry):
+        pl.semaphore_signal(barrier, inc=1, device_id=(peer_a(k),), device_id_type=MESH)
+        pl.semaphore_signal(barrier, inc=1, device_id=(peer_b(k),), device_id_type=MESH)
+        return carry
+
+    lax.fori_loop(1, GROUP, greet, 0, unroll=True)
+    for device in halo_to:
+        pl.semaphore_signal(barrier, inc=1, device_id=(device,), device_id_type=MESH)
+
     loads = []
+    tables = ((part_hbm, part_ref), (slot_hbm, slot_ref), (iface_hbm, iface_ref))
+    for n, (src, dst) in enumerate(tables):
+        loads.append(pltpu.make_async_copy(src, dst, index_sem.at[n]))
+        loads[-1].start()
     for i in range(TILES):
         loads.append(
             pltpu.make_async_copy(
@@ -134,17 +153,6 @@
     for i in range(TILES):
         for n, (src, dst) in enumerate(((k_ref, kbuf), (m_ref, mbuf))):
             pltpu.make_async_copy(src.at[i], dst.at[i], load_sem.at[n, i]).start()
-
-    barrier = pltpu.get_barrier_semaphore()
-
-    def greet(k, carry):
-        pl.semaphore_signal(barrier, inc=1, device_id=(peer_a(k),), device_id_type=MESH)
-        pl.semaphore_signal(barrier, inc=1, device_id=(peer_b(k),), device_id_type=MESH)
-        return carry
-
-    lax.fori_loop(1, GROUP, greet, 0)
-    for device in halo_to:
-        pl.semaphore_signal(barrier, inc=1, device_id=(device,), device_id_type=MESH)
 
     def halo(step, out, into):
         for g, device in enumerate(halo_to):
@@ -176,7 +184,7 @@
             ).start()
             return carry
 
-        lax.fori_loop(1, GROUP, send, 0)
+        lax.fori_loop(1, GROUP, send, 0, unroll=True)
 
     def gathered(buf, stage, step):
         most = buf.at[pl.ds(0, GROUP - 1)]
@@ -186,6 +194,11 @@
             total = total + buf[j]
         return total
 
+    def span(i):
+        return pl.ds(i * WIDTH, WIDTH)
+
+    for copy in loads:
+        copy.wait()
     columns = []
     for i in range(TILES):
         line = []
@@ -200,12 +213,6 @@
             line.append(jnp.where(part == me, slot, where + slot))
         columns.append(line)
     iface = [iface_ref[0], iface_ref[1]]
-
-    def span(i):
-        return pl.ds(i * WIDTH, WIDTH)
-
-    for copy in loads:
-        copy.wait()
     for s in range(2):
         h0out[s] = xt[iface[s]]
     pl.semaphore_wait(barrier, 33)
@@ -274,10 +281,9 @@
     gram = gram[0:48] + gram[48:96]
     with_qx = gram[:, 0:32] + gram[:, 32:64]
     with_x = gram[:, 64:80] + gram[:, 80:96]
-    payload = jnp.concatenate(
-        [with_qx[16:32], with_qx[32:48], with_x[0:16], jnp.zeros((16, 48), F32)], axis=1
-    )
-    spread(ar_big.at[0], 0, 0, payload)
+    alone = jnp.concatenate([with_x[0:16], jnp.zeros((16, 16), F32)], axis=1)
+    payload = jnp.stack([pack4(with_qx[16:32]), pack4(with_qx[32:48]), pack4(alone)])
+    spread(ar_first.at[0], 0, 0, payload)
 
     for i in range(TILES):
         hi, lo = split(words[i, 0:32])
@@ -285,7 +291,6 @@
         ext32[i, 32:64] = lo
         s_hi[i, 0:32] = hi
         s_lo[i, 0:32] = lo
-    spread(ar_big.at[1], 1, 0, gathered(ar_big.at[0], 0, 0))
     halo_wait(1, h1in)
     for g in range(3):
         for s in range(2):
@@ -313,18 +318,19 @@
     for s in range(2):
         h2out[s] = words[iface[s], 32:96]
     halo(2, h2out, h2in)
+    spread(ar_first.at[1], 1, 0, gathered(ar_first.at[0], 0, 0))
     gram = mm_nt(left[...], right[0:64])
     gram = gram[0:64] + gram[64:128]
     gram = gram[:, 0:32] + gram[:, 32:64]
     payload = jnp.concatenate([gram[16 * r : 16 * r + 16] for r in range(4)], axis=1)
-    spread(ar_big.at[2], 0, 1, payload)
+    spread(ar_big.at[0], 0, 1, payload)
     for i in range(TILES):
         hi, lo = split(words[i, 32:96])
         s_hi[i, 32:96] = hi
         s_lo[i, 32:96] = lo
 
-    total = gathered(ar_big.at[1], 1, 0) * scale
-    g_p, g_q, g_xx = total[:, 0:32], total[:, 32:64], total[:, 64:80]
+    total = gathered(ar_first.at[1], 1, 0) * scale
+    g_p, g_q, g_xx = unpack4(total[0]), unpack4(total[1]), unpack4(total[2])[:, 0:16]
     g_pq, g_px = g_p[:, 0:16], g_p[:, 16:32]
     g_qq, g_qx = g_q[:, 0:16], g_q[:, 16:32]
     row_no = lax.broadcasted_iota(jnp.int32, (PAIRS, 2 * PAIRS), 0)
@@ -358,7 +364,7 @@
         ],
         axis=1,
     )
-    spread(ar_big.at[3], 1, 1, gathered(ar_big.at[2], 0, 1))
+    spread(ar_big.at[1], 1, 1, gathered(ar_big.at[0], 0, 1))
     halo_wait(2, h2in)
     for g in range(3):
         for s in range(2):
@@ -380,6 +386,10 @@
         hi, lo = split(p)
         ext16[t, 0:16] = hi
         ext16[t, 16:32] = lo
+
+    def forward(step):
+        got = gathered(ar_small.at[2 * step - 2], 0, step + 1)
+        spread(ar_small.at[2 * step - 1], 1, step + 1, got)
 
     def residual(step, last):
         for i in range(TILES):
@@ -394,6 +404,8 @@
             for s in range(2):
                 out[s] = ad[iface[s]]
             halo(step + 2, out, h3in.at[step - 1])
+        if step == 2:
+            forward(1)
         gram = mm_nt(left[0:32], right[0:64])
         gram = gram[0:16] + gram[16:32]
         gram = gram[:, 0:32] + gram[:, 32:64]
@@ -401,7 +413,7 @@
 
     residual(1, False)
 
-    total = gathered(ar_big.at[3], 1, 1) * scale
+    total = gathered(ar_big.at[1], 1, 1) * scale
     kq, mq = total[:, 32:64], total[:, 96:128]
     kp, mp = total[:, 0:32], total[:, 64:96]
     image = (small(start_p, kp) + small(start_q, kq)) - theta * (
@@ -432,8 +444,8 @@
                 ext16[t, 16:32] = lo
             for t in range(TILES, EXT):
                 pt[t] = pt[t] + combine(coef, 64, t)
-            got = gathered(ar_small.at[2 * step - 2], 0, step + 1)
-            spread(ar_small.at[2 * step - 1], 1, step + 1, got)
+            if step == 2:
+                forward(2)
             halo_wait(step + 2, h3in.at[step - 1])
             for g in range(3):
                 for s in range(2):
@@ -445,8 +457,7 @@
                     ext16[t, 16:32] = lo
             residual(step + 1, step == 2)
         else:
-            got = gathered(ar_small.at[2 * step - 2], 0, step + 1)
-            spread(ar_small.at[2 * step - 1], 1, step + 1, got)
+            forward(3)
             for t in range(TILES):
                 pt[t] = pt[t] - RELAX * ad[t] + combine(coef, 64, t)
         r_px = small(r, g_px)
@@ -472,7 +483,8 @@
             pltpu.make_async_copy(out, out, hs_sem.at[step]).wait()
     for step in range(5):
         for stage in range(2):
-            buf = ar_big.at[2 * step + stage] if step < 2 else ar_small.at[2 * step - 4 + stage]
+            buf = (ar_first, ar_big, ar_small, ar_small, ar_small)[step]
+            buf = buf.at[max(2 * step - 4, 0) + stage]
             most = buf.at[pl.ds(0, GROUP - 1)]
             pltpu.make_async_copy(most, most, as_sem.at[2 * step + stage]).wait()
 
@@ -486,8 +498,7 @@
             jax.ShapeDtypeStruct((PAIRS, LOCAL), F32),
             jax.ShapeDtypeStruct((1, PAIRS), F32),
         ),
-        in_specs=[pl.BlockSpec(memory_space=pl.ANY)] * 3
-        + [pl.BlockSpec(memory_space=pltpu.SMEM)] * 3,
+        in_specs=[pl.BlockSpec(memory_space=pltpu.HBM)] * 6,
         out_specs=(pl.BlockSpec(memory_space=vmem), pl.BlockSpec(memory_space=vmem)),
         scratch_shapes=[
             vmem((TILES, BLOCKS, WIDTH, WIDTH), F32),
@@ -499,7 +510,6 @@
             vmem((EXT, 32, WIDTH), BF16),
             vmem((EXT, 64, WIDTH), BF16),
             vmem((TILES, 96, WIDTH), F32),
-            vmem((8, WIDTH), F32),
             vmem((EXT, 96, WIDTH), BF16),
             vmem((EXT, 96, WIDTH), BF16),
             vmem((EXT, 16, WIDTH), F32),
@@ -514,9 +524,14 @@
             vmem((3, 2, 32, WIDTH), F32),
             vmem((3, 2, 64, WIDTH), F32),
             vmem((2, 3, 2, 16, WIDTH), F32),
-            vmem((4, GROUP, 16, WIDTH), F32),
+            vmem((2, GROUP, 3, 4, WIDTH), F32),
+            vmem((2, GROUP, 16, WIDTH), F32),
             vmem((6, GROUP, 4, WIDTH), F32),
+            pltpu.SMEM((TILES, BLOCKS), jnp.int32),
+            pltpu.SMEM((TILES, BLOCKS), jnp.int32),
+            pltpu.SMEM((2,), jnp.int32),
             pltpu.SemaphoreType.DMA((2, TILES)),
+            pltpu.SemaphoreType.DMA((3,)),
             pltpu.SemaphoreType.DMA((TILES,)),
             pltpu.SemaphoreType.DMA((5,)),
             pltpu.SemaphoreType.DMA((5,)),
@@ -524,7 +539,7 @@
             pltpu.SemaphoreType.DMA((10,)),
         ],
         compiler_params=pltpu.CompilerParams(
-            collective_id=0, has_side_effects=True, vmem_limit_bytes=48 * 1024 * 1024
+            collective_id=0, has_side_effects=True, vmem_limit_bytes=60 * 1024 * 1024
         ),
     )(basis, k_tiles, m_tiles, tile_part, tile_slot, iface_rows)
     return corrections, theta.reshape(PAIRS)

time: 64.2 us -> 57.4 us (0.89)
  local copies, waits for them, and re-layouts: 7.48 us -> 2.59 us
  Pallas kernels: 55.8 us -> 54 us
    unnamed x14 -> x2, local copies, waits for them, and re-layouts: 7.48 us -> 2.59 us
    pallas_call x1, Pallas kernels: 55.8 us -> 54 us  [shards(): pl.pallas_call(functools.partial(kernel, 1.0 / rows), out_shape=(jax.Shap...]
where the time goes in v1:
time: 57.4 us; the launch traced here: 57.2 us
  Pallas kernels  54 us (94%)
  local copies, waits for them, and re-layouts  2.59 us (5%)
  between operations  0.64 us (1%)
    pallas_call x1, Pallas kernels, shards(): pl.pallas_call(functools.partial(kernel, 1.0 / rows), out_shape=(jax.Shap...  54 us
    unnamed x2, local copies, waits for them, and re-layouts  2.59 us

profile of v1, /device:TPU:1, one launch (start us, length us, event | category | flops | bytes accessed | tf_op | source)
XLA Modules:
  0.0 57.2 jit_solution(6232014077354843989)
XLA Ops:
  0.6 54.0 %shard_map.77 = (f32[16,1024]{1,0:T(8,128)}, f32[1,16]{1,0:T(1,128)}) custom-call(f32[16,1024]{1,0:T(8,128)} %basis_ref.1, f32[8,5,128,128]{3,2,1,0:T(8,128)} %k_ref.1, f32[8,5,128,128]{3,2,1,0:T(8,128)} %m_ref.1, s32[8,5]{1,0:T(8,128)} %part_hbm.1, s32[8,5]{1,0:T(8,128)} %slot_hbm.1, s32[2]{0:T(128)} %iface_hbm.1), custom_call_target="tpu_custom_call" | custom-call | tf_op jit(solution)/shard_map/pallas_call | solution.py:495
  54.6 1.5 %copy.10 = f32[16,1024]{1,0:T(8,128)} copy(f32[16,1024]{1,0:T(8,128)} %get-tuple-element.8) | data formatting | bytes 131072
  56.1 1.1 %copy.11 = f32[16]{0:T(128)} copy(f32[16]{0:T(128)} %bitcast.1) | data formatting | bytes 128

commit v2 on v1

--- a/solution.py
+++ b/solution.py
@@ -100,6 +100,12 @@
     ar_first,
     ar_big,
     ar_small,
+    ar_third,
+    ar_extra,
+    back,
+    adj,
+    zin,
+    right2,
     part_ref,
     slot_ref,
     iface_ref,
@@ -291,6 +297,35 @@
         ext32[i, 32:64] = lo
         s_hi[i, 0:32] = hi
         s_lo[i, 0:32] = lo
+    for i in range(TILES):
+        hi, lo = right[0:32, span(i)], right[32:64, span(i)]
+        none = jnp.zeros((32, WIDTH), BF16)
+        hi = jnp.concatenate(
+            [jnp.concatenate([hi, none], axis=1), jnp.concatenate([none, hi], axis=1)], axis=0
+        )
+        lo = jnp.concatenate(
+            [jnp.concatenate([lo, none], axis=1), jnp.concatenate([none, lo], axis=1)], axis=0
+        )
+        high = mm_nt(jnp.concatenate([hi, lo], axis=0), w_hi[i])
+        share = high[0:64] + high[64:128] + mm_nt(hi, w_lo[i])
+        for b in range(BLOCKS):
+            back[i, b] = share[:, b * WIDTH : (b + 1) * WIDTH]
+
+    def collect(j, total):
+        for i in range(TILES):
+            for b in range(1, BLOCKS):
+                total = total + jnp.where(columns[i][b] == j, back[i, b], 0.0)
+        adj[j] = total
+
+    def collect_remote(j, carry):
+        collect(j, jnp.zeros((64, WIDTH), F32))
+        return carry
+
+    def collect_local(j, carry):
+        collect(j, back[j, 0])
+        return carry
+
+    lax.fori_loop(TILES, EXT, collect_remote, 0)
     halo_wait(1, h1in)
     for g in range(3):
         for s in range(2):
@@ -324,10 +359,20 @@
     gram = gram[:, 0:32] + gram[:, 32:64]
     payload = jnp.concatenate([gram[16 * r : 16 * r + 16] for r in range(4)], axis=1)
     spread(ar_big.at[0], 0, 1, payload)
+    for g, device in enumerate((halo_to[1], halo_to[0], halo_to[2])):
+        pltpu.make_async_remote_copy(
+            src_ref=adj.at[pl.ds(TILES + 2 * g, 2)],
+            dst_ref=zin.at[g],
+            send_sem=hs_sem.at[5],
+            recv_sem=hr_sem.at[5],
+            device_id=(device,),
+            device_id_type=MESH,
+        ).start()
     for i in range(TILES):
         hi, lo = split(words[i, 32:96])
         s_hi[i, 32:96] = hi
         s_lo[i, 32:96] = lo
+    lax.fori_loop(0, TILES, collect_local, 0)
 
     total = gathered(ar_first.at[1], 1, 0) * scale
     g_p, g_q, g_xx = unpack4(total[0]), unpack4(total[1]), unpack4(total[2])[:, 0:16]
@@ -387,31 +432,58 @@
         ext16[t, 0:16] = hi
         ext16[t, 16:32] = lo
 
-    def forward(step):
-        got = gathered(ar_small.at[2 * step - 2], 0, step + 1)
-        spread(ar_small.at[2 * step - 1], 1, step + 1, got)
-
-    def residual(step, last):
+    def residual(step):
         for i in range(TILES):
             y = apply(ext16, 16, i)
             image = y[:, :WIDTH] - wide * y[:, WIDTH:]
-            hi, lo = split(image)
-            left[0:16, span(i)] = hi
-            left[16:32, span(i)] = lo
-            ad[i] = image * d[i]
-        if not last:
+            moved = image * d[i]
+            ad[i] = moved
+            if step < 3:
+                hi, lo = split(image)
+                left[0:16, span(i)] = hi
+                left[16:32, span(i)] = lo
+            if step == 2:
+                hi, lo = split(moved)
+                left[32:48, span(i)] = hi
+                left[48:64, span(i)] = lo
+        if step < 3:
             out = h3out.at[step - 1]
             for s in range(2):
                 out[s] = ad[iface[s]]
             halo(step + 2, out, h3in.at[step - 1])
-        if step == 2:
-            forward(1)
-        gram = mm_nt(left[0:32], right[0:64])
-        gram = gram[0:16] + gram[16:32]
-        gram = gram[:, 0:32] + gram[:, 32:64]
-        spread(ar_small.at[2 * step - 2], 0, step + 1, pack4(gram))
-
-    residual(1, False)
+
+    def with_qxd(rows):
+        gram = mm_nt(left[0 : 2 * rows], right[0:64])
+        gram = gram[0:rows] + gram[rows : 2 * rows]
+        return gram[:, 0:32] + gram[:, 32:64]
+
+    def with_back(both, rows):
+        gram = mm_nt(both, right2[...])
+        gram = gram[0:rows] + gram[rows : 2 * rows]
+        return gram[:, 0:64] + gram[:, 64:128]
+
+    residual(1)
+    gram = with_qxd(16)
+    spread(ar_small.at[0], 0, 2, pack4(gram))
+
+    pltpu.make_async_copy(zin, zin, hr_sem.at[5]).wait()
+    for j in range(TILES):
+        total = adj[j]
+        for s in range(2):
+            for g in range(3):
+                total = total + jnp.where(iface[s] == j, zin[g, s], 0.0)
+        hi, lo = split(total)
+        right2[0:64, span(j)] = hi
+        right2[64:128, span(j)] = lo
+    both = jnp.concatenate(
+        [
+            jnp.concatenate([s_hi[t, 32:64] for t in range(TILES)], axis=1),
+            jnp.concatenate([s_lo[t, 32:64] for t in range(TILES)], axis=1),
+        ],
+        axis=0,
+    )
+    gram = with_back(both, 32)
+    spread(ar_extra.at[0], 0, 4, jnp.concatenate([gram[0:16], gram[16:32]], axis=1))
 
     total = gathered(ar_big.at[1], 1, 1) * scale
     kq, mq = total[:, 32:64], total[:, 96:128]
@@ -421,54 +493,77 @@
     )
     p_x = 2.0 * start_x - RELAX * image[:, 16:32] + RELAX * small(r, g_px)
 
-    for step in (1, 2, 3):
+    def advance(image, r_pq, p_x):
         m = small(image[:, 0:16] - r_pq, gram_m)
         c_x = p_x + RELAX * small(m, g_qx)
-        r = small(c_x, gram_v)
-        m_image = RELAX * (small(m, kq) - theta * small(m, mq))
-        coef = jnp.concatenate(
-            [
-                start_p + RELAX * r,
-                start_q + RELAX * m,
-                -RELAX * RELAX * m,
-                RELAX * RELAX * theta * m,
-            ],
-            axis=1,
-        )
-        if step < 3:
-            for t in range(TILES):
-                p = pt[t] - RELAX * ad[t] + combine(coef, 64, t)
+        return m, c_x, small(c_x, gram_v)
+
+    def coefficients(m, r):
+        parts = [
+            start_p + RELAX * r,
+            start_q + RELAX * m,
+            -RELAX * RELAX * m,
+            RELAX * RELAX * theta * m,
+        ]
+        return jnp.concatenate(parts, axis=1)
+
+    def image_of(m):
+        return RELAX * (small(m, kq) - theta * small(m, mq))
+
+    for step in (1, 2):
+        m, c_x, r = advance(image, r_pq, p_x)
+        m_image = image_of(m)
+        coef = coefficients(m, r)
+        for t in range(TILES):
+            p = pt[t] - RELAX * ad[t] + combine(coef, 64, t)
+            pt[t] = p
+            hi, lo = split(p)
+            ext16[t, 0:16] = hi
+            ext16[t, 16:32] = lo
+        for t in range(TILES, EXT):
+            pt[t] = pt[t] + combine(coef, 64, t)
+        if step == 2:
+            spread(ar_third.at[1], 1, 3, gathered(ar_third.at[0], 0, 3))
+        halo_wait(step + 2, h3in.at[step - 1])
+        for g in range(3):
+            for s in range(2):
+                t = TILES + 2 * g + s
+                p = pt[t] - RELAX * h3in[step - 1, g, s]
                 pt[t] = p
                 hi, lo = split(p)
                 ext16[t, 0:16] = hi
                 ext16[t, 16:32] = lo
-            for t in range(TILES, EXT):
-                pt[t] = pt[t] + combine(coef, 64, t)
-            if step == 2:
-                forward(2)
-            halo_wait(step + 2, h3in.at[step - 1])
-            for g in range(3):
-                for s in range(2):
-                    t = TILES + 2 * g + s
-                    p = pt[t] - RELAX * h3in[step - 1, g, s]
-                    pt[t] = p
-                    hi, lo = split(p)
-                    ext16[t, 0:16] = hi
-                    ext16[t, 16:32] = lo
-            residual(step + 1, step == 2)
-        else:
-            forward(3)
-            for t in range(TILES):
-                pt[t] = pt[t] - RELAX * ad[t] + combine(coef, 64, t)
+        residual(step + 1)
         r_px = small(r, g_px)
         r_pq = small(r, g_pq)
-        total = unpack4(gathered(ar_small.at[2 * step - 1], 1, step + 1)) * scale
-        image = total + m_image
-        p_x = c_x + start_x - RELAX * image[:, 16:32] + RELAX * r_px
-
-    m = small(image[:, 0:16] - r_pq, gram_m)
-    c_x = p_x + RELAX * small(m, g_qx)
-    r = small(c_x, gram_v)
+        if step == 1:
+            spread(ar_small.at[1], 1, 2, gathered(ar_small.at[0], 0, 2))
+            gram = with_qxd(16)
+            gram_b = with_back(left[32:64], 16)
+            gram_b = gram_b[:, 0:32] - theta * gram_b[:, 32:64]
+            spread(ar_third.at[0], 0, 3, jnp.stack([pack4(gram), pack4(gram_b)]))
+            spread(ar_extra.at[1], 1, 4, gathered(ar_extra.at[0], 0, 4))
+            image = unpack4(gathered(ar_small.at[1], 1, 2)) * scale + m_image
+            p_x = c_x + start_x - RELAX * image[:, 16:32] + RELAX * r_px
+
+    extra = gathered(ar_extra.at[1], 1, 4) * scale
+    stiff = jnp.concatenate([kp, kq, extra[:, 0:32], extra[:, 64:96]], axis=0)
+    mass = jnp.concatenate([mp, mq, extra[:, 32:64], extra[:, 96:128]], axis=0)
+    known = small(coef, stiff) - theta * small(coef, mass)
+    total = gathered(ar_third.at[1], 1, 3) * scale
+    image = unpack4(total[0])
+    known = known + image - RELAX * unpack4(total[1])
+    image = image + m_image
+    p_x = c_x + start_x - RELAX * image[:, 16:32] + RELAX * r_px
+    m, c_x, r = advance(image, r_pq, p_x)
+    coef = coefficients(m, r)
+    image = known + image_of(m)
+    r_pq = small(r, g_pq)
+    p_x = c_x + start_x - RELAX * image[:, 16:32] + RELAX * small(r, g_px)
+    for t in range(TILES):
+        pt[t] = pt[t] - RELAX * ad[t] + combine(coef, 64, t)
+
+    m, c_x, r = advance(image, r_pq, p_x)
     q_hi, q_lo = split(RELAX * m)
     x_hi, x_lo = split(-r)
     lead = jnp.concatenate([q_hi, x_hi], axis=1)
@@ -481,11 +576,11 @@
     for step, out in enumerate((h0out, h1out, h2out, h3out.at[0], h3out.at[1])):
         for g in range(3):
             pltpu.make_async_copy(out, out, hs_sem.at[step]).wait()
-    for step in range(5):
+    sent = adj.at[pl.ds(TILES, 6)]
+    pltpu.make_async_copy(sent, sent, hs_sem.at[5]).wait()
+    for step, buf in enumerate((ar_first, ar_big, ar_small, ar_third, ar_extra)):
         for stage in range(2):
-            buf = (ar_first, ar_big, ar_small, ar_small, ar_small)[step]
-            buf = buf.at[max(2 * step - 4, 0) + stage]
-            most = buf.at[pl.ds(0, GROUP - 1)]
+            most = buf.at[stage, pl.ds(0, GROUP - 1)]
             pltpu.make_async_copy(most, most, as_sem.at[2 * step + stage]).wait()
 
 
@@ -526,15 +621,21 @@
             vmem((2, 3, 2, 16, WIDTH), F32),
             vmem((2, GROUP, 3, 4, WIDTH), F32),
             vmem((2, GROUP, 16, WIDTH), F32),
-            vmem((6, GROUP, 4, WIDTH), F32),
+            vmem((2, GROUP, 4, WIDTH), F32),
+            vmem((2, GROUP, 2, 4, WIDTH), F32),
+            vmem((2, GROUP, 16, WIDTH), F32),
+            vmem((TILES, BLOCKS, 64, WIDTH), F32),
+            vmem((EXT, 64, WIDTH), F32),
+            vmem((3, 2, 64, WIDTH), F32),
+            vmem((128, LOCAL), BF16),
             pltpu.SMEM((TILES, BLOCKS), jnp.int32),
             pltpu.SMEM((TILES, BLOCKS), jnp.int32),
             pltpu.SMEM((2,), jnp.int32),
             pltpu.SemaphoreType.DMA((2, TILES)),
             pltpu.SemaphoreType.DMA((3,)),
             pltpu.SemaphoreType.DMA((TILES,)),
-            pltpu.SemaphoreType.DMA((5,)),
-            pltpu.SemaphoreType.DMA((5,)),
+            pltpu.SemaphoreType.DMA((6,)),
+            pltpu.SemaphoreType.DMA((6,)),
             pltpu.SemaphoreType.DMA((10,)),
             pltpu.SemaphoreType.DMA((10,)),
         ],

time: 57.4 us -> 53 us (0.923)
  Pallas kernels: 54 us -> 49.7 us
    pallas_call x1, Pallas kernels: 54 us -> 49.7 us  [shards(): pl.pallas_call(functools.partial(kernel, 1.0 / rows), out_shape=(jax.Shap...]
where the time goes in v2:
time: 53 us; the launch traced here: 52.9 us
  Pallas kernels  49.7 us (94%)
  local copies, waits for them, and re-layouts  2.59 us (5%)
  between operations  0.64 us (1%)
    pallas_call x1, Pallas kernels, shards(): pl.pallas_call(functools.partial(kernel, 1.0 / rows), out_shape=(jax.Shap...  49.7 us
    unnamed x2, local copies, waits for them, and re-layouts  2.59 us

profile of v2, /device:TPU:1, one launch (start us, length us, event | category | flops | bytes accessed | tf_op | source)
XLA Modules:
  0.0 52.9 jit_solution(15543250385228450714)
XLA Ops:
  0.6 49.7 %shard_map.77 = (f32[16,1024]{1,0:T(8,128)}, f32[1,16]{1,0:T(1,128)}) custom-call(f32[16,1024]{1,0:T(8,128)} %basis_ref.1, f32[8,5,128,128]{3,2,1,0:T(8,128)} %k_ref.1, f32[8,5,128,128]{3,2,1,0:T(8,128)} %m_ref.1, s32[8,5]{1,0:T(8,128)} %part_hbm.1, s32[8,5]{1,0:T(8,128)} %slot_hbm.1, s32[2]{0:T(128)} %iface_hbm.1), custom_call_target="tpu_custom_call" | custom-call | tf_op jit(solution)/shard_map/pallas_call | solution.py:590
  50.3 1.5 %copy.10 = f32[16,1024]{1,0:T(8,128)} copy(f32[16,1024]{1,0:T(8,128)} %get-tuple-element.8) | data formatting | bytes 131072
  51.8 1.1 %copy.11 = f32[16]{0:T(128)} copy(f32[16]{0:T(128)} %bitcast.1) | data formatting | bytes 128

commit v3 on v2

--- a/solution.py
+++ b/solution.py
@@ -50,6 +50,17 @@
 
 def unpack4(v):
     return jnp.concatenate([v[:, 32 * i : 32 * i + 32] for i in range(4)], axis=0)
+
+
+def pack2(v):
+    flat = jnp.concatenate([v[2 * i : 2 * i + 2] for i in range(8)], axis=1)
+    return jnp.stack([flat[:, WIDTH * u : WIDTH * u + WIDTH] for u in range(v.shape[1] // 16)])
+
+
+def unpack2(v):
+    flat = jnp.concatenate([v[u] for u in range(v.shape[0])], axis=1)
+    wide = 16 * v.shape[0]
+    return jnp.concatenate([flat[:, wide * i : wide * i + wide] for i in range(8)], axis=0)
 
 
 def eliminate(gram, rows, eye):
@@ -287,8 +298,9 @@
     gram = gram[0:48] + gram[48:96]
     with_qx = gram[:, 0:32] + gram[:, 32:64]
     with_x = gram[:, 64:80] + gram[:, 80:96]
-    alone = jnp.concatenate([with_x[0:16], jnp.zeros((16, 16), F32)], axis=1)
-    payload = jnp.stack([pack4(with_qx[16:32]), pack4(with_qx[32:48]), pack4(alone)])
+    payload = pack2(
+        jnp.concatenate([with_qx[16:32], with_qx[32:48], with_x[0:16]], axis=1)
+    )
     spread(ar_first.at[0], 0, 0, payload)
 
     for i in range(TILES):
@@ -326,6 +338,15 @@
         return carry
 
     lax.fori_loop(TILES, EXT, collect_remote, 0)
+    for g, device in enumerate((halo_to[1], halo_to[0], halo_to[2])):
+        pltpu.make_async_remote_copy(
+            src_ref=adj.at[pl.ds(TILES + 2 * g, 2)],
+            dst_ref=zin.at[g],
+            send_sem=hs_sem.at[5],
+            recv_sem=hr_sem.at[5],
+            device_id=(device,),
+            device_id_type=MESH,
+        ).start()
     halo_wait(1, h1in)
     for g in range(3):
         for s in range(2):
@@ -337,6 +358,8 @@
             s_lo[t, 0:32] = lo
 
     for i in range(TILES):
+        if i == 0:
+            spread(ar_first.at[1], 1, 0, gathered(ar_first.at[0], 0, 0))
         y = apply(ext32, 32, i)
         stiff, mass = y[:, :WIDTH], y[:, WIDTH:]
         hi, lo = split(stiff)
@@ -353,29 +376,52 @@
     for s in range(2):
         h2out[s] = words[iface[s], 32:96]
     halo(2, h2out, h2in)
-    spread(ar_first.at[1], 1, 0, gathered(ar_first.at[0], 0, 0))
     gram = mm_nt(left[...], right[0:64])
     gram = gram[0:64] + gram[64:128]
     gram = gram[:, 0:32] + gram[:, 32:64]
-    payload = jnp.concatenate([gram[16 * r : 16 * r + 16] for r in range(4)], axis=1)
+    kept = gram[16:32]
+    payload = pack2(jnp.concatenate([gram[0:16], kept + gram[32:48], gram[48:64]], axis=1))
     spread(ar_big.at[0], 0, 1, payload)
-    for g, device in enumerate((halo_to[1], halo_to[0], halo_to[2])):
-        pltpu.make_async_remote_copy(
-            src_ref=adj.at[pl.ds(TILES + 2 * g, 2)],
-            dst_ref=zin.at[g],
-            send_sem=hs_sem.at[5],
-            recv_sem=hr_sem.at[5],
-            device_id=(device,),
-            device_id_type=MESH,
-        ).start()
     for i in range(TILES):
         hi, lo = split(words[i, 32:96])
         s_hi[i, 32:96] = hi
         s_lo[i, 32:96] = lo
     lax.fori_loop(0, TILES, collect_local, 0)
 
+    def with_back(both, rows):
+        gram = mm_nt(both, right2[...])
+        gram = gram[0:rows] + gram[rows : 2 * rows]
+        return gram[:, 0:64] + gram[:, 64:128]
+
+    pltpu.make_async_copy(zin, zin, hr_sem.at[5]).wait()
+    for j in range(TILES):
+        total = adj[j]
+        for s in range(2):
+            for g in range(3):
+                total = total + jnp.where(iface[s] == j, zin[g, s], 0.0)
+        hi, lo = split(total)
+        right2[0:64, span(j)] = hi
+        right2[64:128, span(j)] = lo
+    both = jnp.concatenate(
+        [
+            jnp.concatenate([s_hi[t, 32:64] for t in range(TILES)], axis=1),
+            jnp.concatenate([s_lo[t, 32:64] for t in range(TILES)], axis=1),
+        ],
+        axis=0,
+    )
+    gram = with_back(both, 32)
+    middle = gram[0:16, 32:64] + gram[16:32, 0:32]
+    spread(
+        ar_extra.at[0],
+        0,
+        4,
+        pack2(jnp.concatenate([gram[0:16, 0:32], middle, gram[16:32, 32:64], kept], axis=1)),
+    )
+
+
     total = gathered(ar_first.at[1], 1, 0) * scale
-    g_p, g_q, g_xx = unpack4(total[0]), unpack4(total[1]), unpack4(total[2])[:, 0:16]
+    total = unpack2(total)
+    g_p, g_q, g_xx = total[:, 0:32], total[:, 32:64], total[:, 64:80]
     g_pq, g_px = g_p[:, 0:16], g_p[:, 16:32]
     g_qq, g_qx = g_q[:, 0:16], g_q[:, 16:32]
     row_no = lax.broadcasted_iota(jnp.int32, (PAIRS, 2 * PAIRS), 0)
@@ -397,7 +443,9 @@
     start_q = RELAX * theta * inv_v
     start_x = small(start_p, g_px) + small(start_q, g_qx)
     r = small(start_x, gram_v)
-    r_pq = small(r, g_pq)
+    pq_m = small(g_pq, gram_m)
+    qx_v = small(g_qx, gram_v)
+    r_m = small(r, pq_m)
     coef = jnp.concatenate(
         [
             2.0 * start_p + RELAX * r,
@@ -409,7 +457,6 @@
         ],
         axis=1,
     )
-    spread(ar_big.at[1], 1, 1, gathered(ar_big.at[0], 0, 1))
     halo_wait(2, h2in)
     for g in range(3):
         for s in range(2):
@@ -434,6 +481,10 @@
 
     def residual(step):
         for i in range(TILES):
+            if i == 4 and step == 1:
+                spread(ar_big.at[1], 1, 1, gathered(ar_big.at[0], 0, 1))
+            if i == 4 and step == 2:
+                spread(ar_small.at[1], 1, 2, gathered(ar_small.at[0], 0, 2))
             y = apply(ext16, 16, i)
             image = y[:, :WIDTH] - wide * y[:, WIDTH:]
             moved = image * d[i]
@@ -457,46 +508,22 @@
         gram = gram[0:rows] + gram[rows : 2 * rows]
         return gram[:, 0:32] + gram[:, 32:64]
 
-    def with_back(both, rows):
-        gram = mm_nt(both, right2[...])
-        gram = gram[0:rows] + gram[rows : 2 * rows]
-        return gram[:, 0:64] + gram[:, 64:128]
-
     residual(1)
     gram = with_qxd(16)
     spread(ar_small.at[0], 0, 2, pack4(gram))
 
-    pltpu.make_async_copy(zin, zin, hr_sem.at[5]).wait()
-    for j in range(TILES):
-        total = adj[j]
-        for s in range(2):
-            for g in range(3):
-                total = total + jnp.where(iface[s] == j, zin[g, s], 0.0)
-        hi, lo = split(total)
-        right2[0:64, span(j)] = hi
-        right2[64:128, span(j)] = lo
-    both = jnp.concatenate(
-        [
-            jnp.concatenate([s_hi[t, 32:64] for t in range(TILES)], axis=1),
-            jnp.concatenate([s_lo[t, 32:64] for t in range(TILES)], axis=1),
-        ],
-        axis=0,
-    )
-    gram = with_back(both, 32)
-    spread(ar_extra.at[0], 0, 4, jnp.concatenate([gram[0:16], gram[16:32]], axis=1))
-
-    total = gathered(ar_big.at[1], 1, 1) * scale
-    kq, mq = total[:, 32:64], total[:, 96:128]
-    kp, mp = total[:, 0:32], total[:, 64:96]
-    image = (small(start_p, kp) + small(start_q, kq)) - theta * (
-        small(start_p, mp) + small(start_q, mq)
+    spread(ar_extra.at[1], 1, 4, gathered(ar_extra.at[0], 0, 4))
+    total = unpack2(gathered(ar_big.at[1], 1, 1)) * scale
+    kp, kq_mp, mq = total[:, 0:32], total[:, 32:64], total[:, 64:96]
+    image = -RELAX * (
+        small(inv_v, kp) - theta * (small(inv_v, kq_mp) - theta * small(inv_v, mq))
     )
     p_x = 2.0 * start_x - RELAX * image[:, 16:32] + RELAX * small(r, g_px)
 
-    def advance(image, r_pq, p_x):
-        m = small(image[:, 0:16] - r_pq, gram_m)
-        c_x = p_x + RELAX * small(m, g_qx)
-        return m, c_x, small(c_x, gram_v)
+    def advance(image, r_m, p_x):
+        m = small(image[:, 0:16], gram_m) - r_m
+        r = small(p_x, gram_v) + RELAX * small(m, qx_v)
+        return m, p_x + RELAX * small(m, g_qx), r
 
     def coefficients(m, r):
         parts = [
@@ -511,8 +538,7 @@
         return RELAX * (small(m, kq) - theta * small(m, mq))
 
     for step in (1, 2):
-        m, c_x, r = advance(image, r_pq, p_x)
-        m_image = image_of(m)
+        m, c_x, r = advance(image, r_m, p_x)
         coef = coefficients(m, r)
         for t in range(TILES):
             p = pt[t] - RELAX * ad[t] + combine(coef, 64, t)
@@ -535,35 +561,42 @@
                 ext16[t, 16:32] = lo
         residual(step + 1)
         r_px = small(r, g_px)
-        r_pq = small(r, g_pq)
+        r_m = small(r, pq_m)
         if step == 1:
-            spread(ar_small.at[1], 1, 2, gathered(ar_small.at[0], 0, 2))
             gram = with_qxd(16)
             gram_b = with_back(left[32:64], 16)
             gram_b = gram_b[:, 0:32] - theta * gram_b[:, 32:64]
             spread(ar_third.at[0], 0, 3, jnp.stack([pack4(gram), pack4(gram_b)]))
-            spread(ar_extra.at[1], 1, 4, gathered(ar_extra.at[0], 0, 4))
+            extra = unpack2(gathered(ar_extra.at[1], 1, 4)) * scale
+            kq = extra[:, 96:128]
+            mp = kq_mp - kq
+            m_image = image_of(m)
             image = unpack4(gathered(ar_small.at[1], 1, 2)) * scale + m_image
             p_x = c_x + start_x - RELAX * image[:, 16:32] + RELAX * r_px
 
-    extra = gathered(ar_extra.at[1], 1, 4) * scale
-    stiff = jnp.concatenate([kp, kq, extra[:, 0:32], extra[:, 64:96]], axis=0)
-    mass = jnp.concatenate([mp, mq, extra[:, 32:64], extra[:, 96:128]], axis=0)
-    known = small(coef, stiff) - theta * small(coef, mass)
+    m_image = image_of(m)
+    near = coef[:, 0:32]
+    twice = small(m, extra[:, 0:32]) - theta * (
+        small(m, extra[:, 32:64]) - theta * small(m, extra[:, 64:96])
+    )
+    known = small(near, jnp.concatenate([kp, kq], axis=0)) - theta * small(
+        near, jnp.concatenate([mp, mq], axis=0)
+    )
+    known = known - RELAX * RELAX * twice
     total = gathered(ar_third.at[1], 1, 3) * scale
     image = unpack4(total[0])
     known = known + image - RELAX * unpack4(total[1])
     image = image + m_image
     p_x = c_x + start_x - RELAX * image[:, 16:32] + RELAX * r_px
-    m, c_x, r = advance(image, r_pq, p_x)
+    m, c_x, r = advance(image, r_m, p_x)
     coef = coefficients(m, r)
     image = known + image_of(m)
-    r_pq = small(r, g_pq)
+    r_m = small(r, pq_m)
     p_x = c_x + start_x - RELAX * image[:, 16:32] + RELAX * small(r, g_px)
     for t in range(TILES):
         pt[t] = pt[t] - RELAX * ad[t] + combine(coef, 64, t)
 
-    m, c_x, r = advance(image, r_pq, p_x)
+    m, c_x, r = advance(image, r_m, p_x)
     q_hi, q_lo = split(RELAX * m)
     x_hi, x_lo = split(-r)
     lead = jnp.concatenate([q_hi, x_hi], axis=1)
@@ -590,8 +623,8 @@
     corrections, theta = pl.pallas_call(
         functools.partial(kernel, 1.0 / rows),
         out_shape=(
-            jax.ShapeDtypeStruct((PAIRS, LOCAL), F32),
-            jax.ShapeDtypeStruct((1, PAIRS), F32),
+            pltpu.VMEM((PAIRS, LOCAL), F32),
+            pltpu.VMEM((1, PAIRS), F32),
         ),
         in_specs=[pl.BlockSpec(memory_space=pltpu.HBM)] * 6,
         out_specs=(pl.BlockSpec(memory_space=vmem), pl.BlockSpec(memory_space=vmem)),
@@ -619,11 +652,11 @@
             vmem((3, 2, 32, WIDTH), F32),
             vmem((3, 2, 64, WIDTH), F32),
             vmem((2, 3, 2, 16, WIDTH), F32),
-            vmem((2, GROUP, 3, 4, WIDTH), F32),
-            vmem((2, GROUP, 16, WIDTH), F32),
+            vmem((2, GROUP, 5, 2, WIDTH), F32),
+            vmem((2, GROUP, 6, 2, WIDTH), F32),
             vmem((2, GROUP, 4, WIDTH), F32),
             vmem((2, GROUP, 2, 4, WIDTH), F32),
-            vmem((2, GROUP, 16, WIDTH), F32),
+            vmem((2, GROUP, 8, 2, WIDTH), F32),
             vmem((TILES, BLOCKS, 64, WIDTH), F32),
             vmem((EXT, 64, WIDTH), F32),
             vmem((3, 2, 64, WIDTH), F32),

time: 53 us -> 50.3 us (0.949)
  local copies, waits for them, and re-layouts: 2.59 us -> 1.14 us
  Pallas kernels: 49.7 us -> 48.3 us
    unnamed x2, local copies, waits for them, and re-layouts: 2.59 us -> 1.14 us
    pallas_call x1, Pallas kernels: 49.7 us -> 48.3 us  [shards(): pl.pallas_call(functools.partial(kernel, 1.0 / rows), out_shape=(pltpu.VM...]
where the time goes in v3:
time: 50.3 us; the launch traced here: 50.1 us
  Pallas kernels  48.3 us (96%)
  local copies, waits for them, and re-layouts  1.14 us (2%)
  between operations  0.64 us (1%)
    pallas_call x1, Pallas kernels, shards(): pl.pallas_call(functools.partial(kernel, 1.0 / rows), out_shape=(pltpu.VM...  48.3 us
    unnamed x2, local copies, waits for them, and re-layouts  1.14 us

profile of v3, /device:TPU:1, one launch (start us, length us, event | category | flops | bytes accessed | tf_op | source)
XLA Modules:
  0.0 50.1 jit_solution(8079734129939875394)
XLA Ops:
  0.6 48.3 %shard_map.77 = (f32[16,1024]{1,0:T(8,128)S(1)}, f32[1,16]{1,0:T(1,128)S(1)}) custom-call(f32[16,1024]{1,0:T(8,128)} %basis_ref.1, f32[8,5,128,128]{3,2,1,0:T(8,128)} %k_ref.1, f32[8,5,128,128]{3,2,1,0:T(8,128)} %m_ref.1, s32[8,5]{1,0:T(8,128)} %part_hbm.1, s32[8,5]{1,0:T(8,128)} %slot_hbm.1, s32[2]{0:T(128)} %iface_hbm.1), custom_call_target="tpu_custom_call" | custom-call | tf_op jit(solution)/shard_map/pallas_call | solution.py:623
  49.0 0.6 %copy.10 = f32[16,1024]{1,0:T(8,128)} copy(f32[16,1024]{1,0:T(8,128)S(1)} %get-tuple-element.6) | data formatting | bytes 131072
  49.6 0.5 %copy.11 = f32[16]{0:T(128)} copy(f32[16]{0:T(128)S(1)} %bitcast.1) | data formatting | bytes 128

commit v4 on v3

--- a/solution.py
+++ b/solution.py
@@ -19,6 +19,8 @@
 EXT = TILES + 6
 RELAX = 0.4
 MESH = pl.DeviceIdType.MESH
+ORDER_A = (8, 7, 9, 6, 10, 5, 11, 4, 12, 3, 13, 2, 14, 1, 15)
+ORDER_B = (10, 6, 14, 9, 11, 2, 8, 5, 7, 13, 15, 1, 3, 4, 12)
 F32 = jnp.float32
 BF16 = jnp.bfloat16
 NT = (((1,), (1,)), ((), ()))
@@ -142,16 +144,15 @@
         return base_a + lax.rem(rank_a + k, GROUP)
 
     def peer_b(k):
-        return rank_a + GROUP * lax.rem(rank_b + k, GROUP)
+        across = lax.rem(lax.rem(rank_b, 4) + k % 4, 4)
+        along = lax.rem(rank_b // 4 + k // 4, 4)
+        return rank_a + GROUP * (4 * along + across)
 
     barrier = pltpu.get_barrier_semaphore()
 
-    def greet(k, carry):
-        pl.semaphore_signal(barrier, inc=1, device_id=(peer_a(k),), device_id_type=MESH)
-        pl.semaphore_signal(barrier, inc=1, device_id=(peer_b(k),), device_id_type=MESH)
-        return carry
-
-    lax.fori_loop(1, GROUP, greet, 0, unroll=True)
+    for near, far in zip(ORDER_A, ORDER_B):
+        for device in (peer_b(far), peer_a(near)):
+            pl.semaphore_signal(barrier, inc=1, device_id=(device,), device_id_type=MESH)
     for device in halo_to:
         pl.semaphore_signal(barrier, inc=1, device_id=(device,), device_id_type=MESH)
 
@@ -190,7 +191,7 @@
         peer = peer_a if stage == 0 else peer_b
         buf[rank] = value
 
-        def send(k, carry):
+        for k in ORDER_A if stage == 0 else ORDER_B:
             pltpu.make_async_remote_copy(
                 src_ref=buf.at[rank],
                 dst_ref=buf.at[rank],
@@ -199,9 +200,6 @@
                 device_id=(peer(k),),
                 device_id_type=MESH,
             ).start()
-            return carry
-
-        lax.fori_loop(1, GROUP, send, 0, unroll=True)
 
     def gathered(buf, stage, step):
         most = buf.at[pl.ds(0, GROUP - 1)]

time: 50.3 us -> 49.8 us (0.990)
  no operation moved by 1% of the time
where the time goes in v4:
time: 49.8 us; the launch traced here: 49.7 us
  Pallas kernels  47.9 us (96%)
  local copies, waits for them, and re-layouts  1.14 us (2%)
  between operations  0.64 us (1%)
    pallas_call x1, Pallas kernels, shards(): pl.pallas_call(functools.partial(kernel, 1.0 / rows), out_shape=(pltpu.VM...  47.9 us
    unnamed x2, local copies, waits for them, and re-layouts  1.14 us

profile of v4, /device:TPU:1, one launch (start us, length us, event | category | flops | bytes accessed | tf_op | source)
XLA Modules:
  0.0 49.7 jit_solution(15106944234486449704)
XLA Ops:
  0.6 47.9 %shard_map.77 = (f32[16,1024]{1,0:T(8,128)S(1)}, f32[1,16]{1,0:T(1,128)S(1)}) custom-call(f32[16,1024]{1,0:T(8,128)} %basis_ref.1, f32[8,5,128,128]{3,2,1,0:T(8,128)} %k_ref.1, f32[8,5,128,128]{3,2,1,0:T(8,128)} %m_ref.1, s32[8,5]{1,0:T(8,128)} %part_hbm.1, s32[8,5]{1,0:T(8,128)} %slot_hbm.1, s32[2]{0:T(128)} %iface_hbm.1), custom_call_target="tpu_custom_call" | custom-call | tf_op jit(solution)/shard_map/pallas_call | solution.py:621
  48.5 0.6 %copy.10 = f32[16,1024]{1,0:T(8,128)} copy(f32[16,1024]{1,0:T(8,128)S(1)} %get-tuple-element.6) | data formatting | bytes 131072
  49.2 0.5 %copy.11 = f32[16]{0:T(128)} copy(f32[16]{0:T(128)S(1)} %bitcast.1) | data formatting | bytes 128

commit v5 on v4

--- a/solution.py
+++ b/solution.py
@@ -148,14 +148,6 @@
         along = lax.rem(rank_b // 4 + k // 4, 4)
         return rank_a + GROUP * (4 * along + across)
 
-    barrier = pltpu.get_barrier_semaphore()
-
-    for near, far in zip(ORDER_A, ORDER_B):
-        for device in (peer_b(far), peer_a(near)):
-            pl.semaphore_signal(barrier, inc=1, device_id=(device,), device_id_type=MESH)
-    for device in halo_to:
-        pl.semaphore_signal(barrier, inc=1, device_id=(device,), device_id_type=MESH)
-
     loads = []
     tables = ((part_hbm, part_ref), (slot_hbm, slot_ref), (iface_hbm, iface_ref))
     for n, (src, dst) in enumerate(tables):
@@ -168,6 +160,14 @@
             )
         )
         loads[-1].start()
+    barrier = pltpu.get_barrier_semaphore()
+
+    for near, far in zip(ORDER_A, ORDER_B):
+        for device in (peer_b(far), peer_a(near)):
+            pl.semaphore_signal(barrier, inc=1, device_id=(device,), device_id_type=MESH)
+    for device in halo_to:
+        pl.semaphore_signal(barrier, inc=1, device_id=(device,), device_id_type=MESH)
+
     for i in range(TILES):
         for n, (src, dst) in enumerate(((k_ref, kbuf), (m_ref, mbuf))):
             pltpu.make_async_copy(src.at[i], dst.at[i], load_sem.at[n, i]).start()

time: 49.8 us -> 49.2 us (0.988)
  Pallas kernels: 47.9 us -> 47.3 us
    pallas_call x1, Pallas kernels: 47.9 us -> 47.3 us  [shards(): pl.pallas_call(functools.partial(kernel, 1.0 / rows), out_shape=(pltpu.VM...]
where the time goes in v5:
time: 49.2 us; the launch traced here: 49.1 us
  Pallas kernels  47.3 us (96%)
  local copies, waits for them, and re-layouts  1.14 us (2%)
  between operations  0.64 us (1%)
    pallas_call x1, Pallas kernels, shards(): pl.pallas_call(functools.partial(kernel, 1.0 / rows), out_shape=(pltpu.VM...  47.3 us
    unnamed x2, local copies, waits for them, and re-layouts  1.14 us

profile of v5, /device:TPU:1, one launch (start us, length us, event | category | flops | bytes accessed | tf_op | source)
XLA Modules:
  0.0 49.1 jit_solution(2885050657925874389)
XLA Ops:
  0.6 47.3 %shard_map.77 = (f32[16,1024]{1,0:T(8,128)S(1)}, f32[1,16]{1,0:T(1,128)S(1)}) custom-call(f32[16,1024]{1,0:T(8,128)} %basis_ref.1, f32[8,5,128,128]{3,2,1,0:T(8,128)} %k_ref.1, f32[8,5,128,128]{3,2,1,0:T(8,128)} %m_ref.1, s32[8,5]{1,0:T(8,128)} %part_hbm.1, s32[8,5]{1,0:T(8,128)} %slot_hbm.1, s32[2]{0:T(128)} %iface_hbm.1), custom_call_target="tpu_custom_call" | custom-call | tf_op jit(solution)/shard_map/pallas_call | solution.py:621
  48.0 0.6 %copy.10 = f32[16,1024]{1,0:T(8,128)} copy(f32[16,1024]{1,0:T(8,128)S(1)} %get-tuple-element.6) | data formatting | bytes 131072
  48.6 0.5 %copy.11 = f32[16]{0:T(128)} copy(f32[16]{0:T(128)S(1)} %bitcast.1) | data formatting | bytes 128
